TPU v7x, 32 devices: a whole 2x2x4 slice. The times are simulated.
32 devices in a mesh: dp: 4 (over x, core), pp: 8 (over z, y).
Axes of the slice: x: 2, y: 2, z: 4, core: 2. Of those that a mesh axis runs over, the one named last changes fastest.
Arguments:
- hidden: bfloat16 [512, 4096], P(('dp', 'pp')), may hold values from -400 to 400
- norm_gain: float32 [4096], replicated, may hold values from 0.1 to 1.9
- head: bfloat16 [32768, 4096], P(('dp', 'pp')), may hold values from -32 to 32
- targets: int32 [512], P(('dp', 'pp')), may hold values from 0 to 32767
- route: int32 [32], replicated, may hold values from 0 to 3
Outputs:
- token_loss: float32 [512], P(('dp', 'pp'))
- pipe_loss: float32 [4], replicated
All inputs are finite; a program needn't handle non-finite values.
Results may differ from a plain program's by a relative error of at most 0.00053.
Values may be sent and summed in bfloat16 or wider, within the bound.
A program may use at most 64 MiB of HBM per device.

v0:
```python
import math

import jax
import jax.numpy as jnp
from jax import lax
from jax.sharding import PartitionSpec as P


def rms_normal(rows, gain):
    wide = rows.astype(jnp.float32)
    factor = lax.rsqrt(jnp.mean(wide * wide, axis=1, keepdims=True) + 1e-05)
    return (wide * factor * gain).astype(jnp.bfloat16)


def tile_stats(normed, labels, head, first):
    total = normed.shape[0]
    block = math.gcd(total, 512)
    columns = first + lax.iota(jnp.int32, head.shape[0])

    def one_block(pair):
        rows, marks = pair
        logits = lax.dot_general(
            rows, head, (((1,), (1,)), ((), ())), preferred_element_type=jnp.float32
        )
        peak = jnp.max(logits, axis=1)
        mass = jnp.sum(jnp.exp(logits - peak[:, None]), axis=1)
        hit = jnp.sum(jnp.where(marks[:, None] == columns[None, :], logits, 0.0), axis=1)
        return (peak, mass, hit)

    peak, mass, hit = lax.map(
        one_block,
        (
            normed.reshape(total // block, block, normed.shape[1]),
            labels.reshape(total // block, block),
        ),
    )
    return (peak.reshape(total), mass.reshape(total), hit.reshape(total))


def shards(hidden, norm_gain, head, targets, route):
    place = lax.axis_index(("dp", "pp"))
    devices = lax.axis_size(("dp", "pp"))
    pipes = lax.axis_size("dp")
    rows = hidden.shape[0]
    gathered, labels = (
        lax.all_gather(hidden, ("dp", "pp"), axis=0, tiled=True),
        lax.all_gather(targets, ("dp", "pp"), axis=0, tiled=True),
    )
    normed = rms_normal(gathered, norm_gain)
    peak, mass, hit = tile_stats(normed, labels, head, place * head.shape[0])
    peak_all, mass_all, hit_all = (
        lax.all_to_all(
            peak.reshape(devices, rows), ("dp", "pp"), split_axis=0, concat_axis=0, tiled=True
        ),
        lax.all_to_all(
            mass.reshape(devices, rows), ("dp", "pp"), split_axis=0, concat_axis=0, tiled=True
        ),
        lax.all_to_all(
            hit.reshape(devices, rows), ("dp", "pp"), split_axis=0, concat_axis=0, tiled=True
        ),
    )
    top = jnp.max(peak_all, axis=0)
    mass_own = jnp.sum(mass_all * jnp.exp(peak_all - top[None, :]), axis=0)
    hit_own = jnp.sum(hit_all, axis=0)
    token_loss = top + jnp.log(mass_own) - hit_own
    mine = route[place]
    credit = jnp.where(lax.iota(jnp.int32, pipes) == mine, jnp.sum(token_loss), 0.0)
    summed = lax.psum(credit, ("dp", "pp"))
    pipe_loss = summed / (rows * devices // pipes)
    return (token_loss, pipe_loss)


def solution(mesh):
    placed = (P(("dp", "pp"), None), P(), P(("dp", "pp"), None), P(("dp", "pp")), P())
    return jax.shard_map(
        shards, mesh=mesh, in_specs=placed, out_specs=(P(("dp", "pp")), P()), check_vma=False
    )
```

profile of v0, /device:TPU:0, one launch (start us, length us, event | category | flops | bytes accessed | tf_op | source)
XLA Modules:
  0.0 165.2 jit_solution(11259137968374212607)
XLA Ops:
  7.2 0.0 copy-start.1
  7.2 0.0 all-gather.2.cloned.1.call-start
  7.2 0.7 all-gather.2.cloned.1.call-update
  7.9 0.9 dynamic-update-slice
  8.8 42.0 %all-reduce = s32[512]{0:T(512)S(1)} all-reduce(s32[512]{0:T(512)S(1)} %dynamic-update-slice), channel_id=1, replica_groups=mesh['dp'=4,'pp'=8] {'dp','pp'}, use_global_device_ids=true, to_apply=%add | all-reduce | flops 512 | bytes 4096
  50.8 24.9 %all-gather.2.cloned.1.call-done = bf16[512,4096]{1,0:T(8,128)(2,1)} async-done(((bf16[16,4096]{1,0:T(8,128)(2,1)}), bf16[512,4096]{1,0:T(8,128)(2,1)}) %all-gather.2.cloned.1.call-update) | async-done | bytes 4194320 | tf_op jit(solution)/shard_map/all_gather | solution.py:46
  75.7 0.0 copy-start
  75.7 3.2 %fusion = f32[512]{0:T(512)S(1)} fusion(bf16[512,4096]{1,0:T(8,128)(2,1)} %all-gather.2.cloned.1.call-done), kind=kLoop, calls=%fused_computation.2 | loop fusion | flops 6290944 | bytes 4196352 | tf_op jit(solution)/shard_map/reduce_sum | solution.py:11
  79.0 0.0 copy-done.1
  79.0 0.2 copy-done
  79.2 0.0 copy-start.2
  79.2 7.4 %fusion.8 = (f32[512]{0:T(512)S(1)}, f32[512,1024]{1,0:T(8,128)S(1)}) fusion(bf16[1024,4096]{1,0:T(8,128)(2,1)} %param.7, bf16[512,4096]{1,0:T(8,128)(2,1)S(1)} %copy-done, f32[4096]{0:T(1024)S(1)} %copy-done.1, f32[512]{0:T(512)S(1)} %add_rsqrt_fusion), kind=kOutput, calls=%fused_computation.17 | convolution fusion | flops 4303879680 | bytes 14700544 | tf_op jit(solution)/shard_map/while/body/eval_jaxpr/dot_general | solution.py:22
  86.6 0.7 all_to_all.22
  87.3 3.4 %all-to-all-start = ((f32[32,1,16]{2,1,0:T(1,128)}), f32[32,1,16]{2,1,0:T(1,128)S(1)}, u32[]{:S(2)}, u32[]{:S(2)}) async-start(f32[32,1,16]{2,1,0:T(1,128)} %bitcast), calls=%async_computation | async-start | bytes 32768 | tf_op jit(solution)/shard_map/all_to_all | solution.py:52
  90.7 0.6 exponential_reduce_fusion
  91.3 0.7 all_to_all.24
  92.0 5.8 %all-to-all-done = f32[32,1,16]{2,1,0:T(1,128)S(1)} async-done(((f32[32,1,16]{2,1,0:T(1,128)}), f32[32,1,16]{2,1,0:T(1,128)S(1)}, u32[]{:S(2)}, u32[]{:S(2)}) %all-to-all-start) | async-done | bytes 2080 | tf_op jit(solution)/shard_map/all_to_all | solution.py:52
  97.9 2.6 %all-to-all-start.1 = ((f32[32,1,16]{2,1,0:T(1,128)}), f32[32,1,16]{2,1,0:T(1,128)S(1)}, u32[]{:S(2)}, u32[]{:S(2)}) async-start(f32[32,1,16]{2,1,0:T(1,128)} %bitcast.1), calls=%async_computation.1 | async-start | bytes 32768 | tf_op jit(solution)/shard_map/all_to_all | solution.py:55
  100.4 0.0 copy-done.2
  100.4 0.6 dynamic_slice.9
  101.1 0.7 all_to_all.28
  101.7 0.1 reduce_max.20
  101.8 5.8 %all-to-all-done.1 = f32[32,1,16]{2,1,0:T(1,128)S(1)} async-done(((f32[32,1,16]{2,1,0:T(1,128)}), f32[32,1,16]{2,1,0:T(1,128)S(1)}, u32[]{:S(2)}, u32[]{:S(2)}) %all-to-all-start.1) | async-done | bytes 2080 | tf_op jit(solution)/shard_map/all_to_all | solution.py:55
  107.6 2.5 %all-to-all-start.2 = ((f32[32,1,16]{2,1,0:T(1,128)}), f32[32,1,16]{2,1,0:T(1,128)S(1)}, u32[]{:S(2)}, u32[]{:S(2)}) async-start(f32[32,1,16]{2,1,0:T(1,128)} %bitcast.4), calls=%async_computation.2 | async-start | bytes 32768 | tf_op jit(solution)/shard_map/all_to_all | solution.py:58
  110.1 7.1 %all-to-all-done.2 = f32[32,1,16]{2,1,0:T(1,128)S(1)} async-done(((f32[32,1,16]{2,1,0:T(1,128)}), f32[32,1,16]{2,1,0:T(1,128)S(1)}, u32[]{:S(2)}, u32[]{:S(2)}) %all-to-all-start.2) | async-done | bytes 2080 | tf_op jit(solution)/shard_map/all_to_all | solution.py:58
  117.2 0.1 reduce_sum.60
  117.3 1.1 fusion.7
  118.4 1.3 compare_select_fusion
  119.7 38.2 %psum.7 = f32[4]{0:T(128)S(1)} all-reduce(f32[4]{0:T(128)S(1)} %compare_select_fusion), channel_id=1, replica_groups=mesh['dp'=4,'pp'=8] {'dp','pp'}, use_global_device_ids=true, to_apply=%region_8.9 | all-reduce | flops 4 | bytes 32 | tf_op jit(solution)/shard_map/psum | solution.py:68
  157.9 0.5 broadcast_multiply_fusion
  (4 shorter events, 0.0 us)
Async XLA Ops:
  7.2 71.8 %copy-start.1 = (f32[4096]{0:T(1024)S(1)}, f32[4096]{0:T(1024)}, u32[]{:S(2)}) copy-start(f32[4096]{0:T(1024)} %param.6) | copy-start | bytes 49156
  7.2 68.6 %all-gather.2.cloned.1.call-start = ((), (), s32[]{:S(2)}) async-start(), calls=%async_computation.3 | async-start | bytes 4325376 | tf_op jit(solution)/shard_map/all_gather | solution.py:46
  75.7 3.4 %copy-start = (bf16[512,4096]{1,0:T(8,128)(2,1)S(1)}, bf16[512,4096]{1,0:T(8,128)(2,1)}, u32[]{:S(2)}) copy-start(bf16[512,4096]{1,0:T(8,128)(2,1)} %all-gather.2.cloned.1.call-done) | copy-start | bytes 12582916
  79.2 21.2 %copy-start.2 = (s32[32]{0:T(128)S(1)}, s32[32]{0:T(128)}, u32[]{:S(2)}) copy-start(s32[32]{0:T(128)} %param.9) | copy-start | bytes 388
  87.3 10.5 %all-to-all-start = ((f32[32,1,16]{2,1,0:T(1,128)}), f32[32,1,16]{2,1,0:T(1,128)S(1)}, u32[]{:S(2)}, u32[]{:S(2)}) async-start(f32[32,1,16]{2,1,0:T(1,128)} %bitcast), calls=%async_computation | async-start | bytes 32768 | tf_op jit(solution)/shard_map/all_to_all | solution.py:52
  97.9 9.7 %all-to-all-start.1 = ((f32[32,1,16]{2,1,0:T(1,128)}), f32[32,1,16]{2,1,0:T(1,128)S(1)}, u32[]{:S(2)}, u32[]{:S(2)}) async-start(f32[32,1,16]{2,1,0:T(1,128)} %bitcast.1), calls=%async_computation.1 | async-start | bytes 32768 | tf_op jit(solution)/shard_map/all_to_all | solution.py:55
  107.6 9.6 %all-to-all-start.2 = ((f32[32,1,16]{2,1,0:T(1,128)}), f32[32,1,16]{2,1,0:T(1,128)S(1)}, u32[]{:S(2)}, u32[]{:S(2)}) async-start(f32[32,1,16]{2,1,0:T(1,128)} %bitcast.4), calls=%async_computation.2 | async-start | bytes 32768 | tf_op jit(solution)/shard_map/all_to_all | solution.py:58
Sparse Core Ops, SparseCore 0:
  11.1 64.6 all-gather.1
where the time goes:
time: 166 us; the launch traced here: 165 us
  blocking collectives  80.3 us (48%)
  waiting for transfers between devices  44.3 us (27%)
  between operations  14.1 us (8%)
  starting transfers between devices  8.47 us (5%)
  matrix products  7.43 us (4%)
  other arithmetic  6.91 us (4%)
  local copies, waits for them, and re-layouts  3.72 us (2%)
    unnamed x1, blocking collectives  42 us
    psum x1, blocking collectives, shards(): summed = lax.psum(credit, ('dp', 'pp'))  38.2 us
    all_gather x1, waiting for transfers between devices, shards(): lax.all_gather(hidden, ('dp', 'pp'), axis=0, tiled=True)  24.9 us
    dot_general x1, matrix products, one_block(): lax.dot_general(rows, head, (((1,), (1,)), ((), ())), preferred_element_t...  7.43 us
    all_to_all x1, waiting for transfers between devices, shards(): lax.all_to_all(hit.reshape(devices, rows), ('dp', 'pp'), split_axis=0, co...  7.12 us
    all_to_all x1, waiting for transfers between devices, shards(): lax.all_to_all(peak.reshape(devices, rows), ('dp', 'pp'), split_axis=0, c...  5.84 us
    all_to_all x1, waiting for transfers between devices, shards(): lax.all_to_all(mass.reshape(devices, rows), ('dp', 'pp'), split_axis=0, c...  5.78 us
    all_to_all x1, starting transfers between devices, shards(): lax.all_to_all(peak.reshape(devices, rows), ('dp', 'pp'), split_axis=0, c...  3.39 us
  transfers between devices with their start and end apart: 4, of which 4 were waited for; matrix products, arithmetic and copies ran while one was open for 1% of the time, Pallas kernels for 0%

commit v1 on v0

v1 whole, which is shorter than its diff:
```python
import functools
import math

import jax
import jax.numpy as jnp
from jax import lax
from jax.experimental import pallas as pl
from jax.experimental.pallas import tpu as pltpu
from jax.sharding import PartitionSpec as P

CORES = 2
MESH = pl.DeviceIdType.MESH


def kernel(geom, hid, gain, tgt, route, head, out, g, hbuf, stat, loss_ref, rmap,
           recv, sends, stat_send, stat_recv, head_sem):
    nx, ny, nz, ndp, npp = geom
    devices = ndp * npp
    rows, depth = hid.shape
    half_depth = depth // 2
    width = g.shape[1]
    columns = nx * ny
    lanes = nz * CORES * rows
    vocab = hbuf.shape[0]
    vt = math.gcd(vocab, 256)

    dp, pp = lax.axis_index("dp"), lax.axis_index("pp")
    me = dp * npp + pp
    c, x = lax.rem(dp, CORES), dp // CORES
    y, z = lax.rem(pp, ny), pp // ny

    def pos_of(xx, yy, zz, cc):
        return ((xx * ny + yy) * nz + zz) * CORES + cc

    def device(xx, yy, zz, cc):
        return (xx * CORES + cc, zz * ny + yy)

    barrier = pltpu.get_barrier_semaphore()

    def greet(d, carry):
        other = lax.rem(me + d, devices)
        pl.semaphore_signal(barrier, inc=1, device_id=(other // npp, lax.rem(other, npp)),
                            device_id_type=MESH)
        return carry

    lax.fori_loop(1, devices, greet, 0)
    head_copy = pltpu.make_async_copy(head, hbuf, head_sem)
    head_copy.start()

    mine = pos_of(x, y, z, c)
    own = pl.ds(pl.multiple_of(mine * rows, rows), rows)
    wide = hid[...].astype(jnp.float32)
    factor = lax.rsqrt(jnp.mean(wide * wide, axis=1, keepdims=True) + 1e-05)
    g[own, 0:depth] = (wide * factor * gain[...]).astype(jnp.bfloat16)
    marks = jnp.broadcast_to(tgt[...], (rows, rows))
    square = (rows, rows)
    eye = lax.broadcasted_iota(jnp.int32, square, 0) == lax.broadcasted_iota(jnp.int32, square, 1)
    mark = jnp.sum(jnp.where(eye, marks, 0).astype(jnp.float32), axis=1, keepdims=True)
    high = jnp.floor(mark / 65536.0)
    rest = mark - high * 65536.0
    mid = jnp.floor(rest / 256.0)
    low = rest - mid * 256.0
    lane = lax.broadcasted_iota(jnp.int32, (rows, width - depth), 1)
    digits = jnp.where(lane == 0, low, jnp.where(lane == 1, mid, jnp.where(lane == 2, high, 0.0)))
    g[own, depth:width] = digits.astype(jnp.bfloat16)

    col = lax.broadcasted_iota(jnp.int32, (columns, lanes), 0)
    block = lax.broadcasted_iota(jnp.int32, (columns, lanes), 1) // rows
    where = col * (nz * CORES) + block
    relay = jnp.zeros((columns, lanes), jnp.int32)
    for d in range(devices):
        ddp, dpp = d // npp, d % npp
        there = pos_of(ddp // CORES, dpp % ny, dpp // ny, ddp % CORES)
        relay = jnp.where(where == there, route[d], relay)
    rmap[...] = relay

    pl.semaphore_wait(barrier, devices - 1)

    def piece(pos, half):
        part = pl.ds(0, half_depth) if half == 0 else pl.ds(half_depth, width - half_depth)
        return g.at[pl.ds(pl.multiple_of(pos * rows, rows), rows), part]

    def copy(pos, half, kind, target):
        return pltpu.make_async_remote_copy(
            src_ref=piece(pos, half),
            dst_ref=piece(pos, half),
            send_sem=sends.at[kind, half, pos // CORES],
            recv_sem=recv.at[half, pos],
            device_id=target,
            device_id_type=MESH,
        )

    partner = device(x, y, z, 1 - c)
    up, down = device(x, y, z + 1, c), device(x, y, z - 1, c)
    next_x = device(lax.rem(x + 1, nx), y, z, c)
    next_y = device(x, lax.rem(y + 1, ny), z, c)

    def arrive(half, f, s, k, sign, act):
        if half == 0:
            xx, yy = lax.rem(x - f + nx, nx), lax.rem(y - s + ny, ny)
            first, second, nf, ns = next_x, next_y, nx, ny
        else:
            xx, yy = lax.rem(x - s + nx, nx), lax.rem(y - f + ny, ny)
            first, second, nf, ns = next_y, next_x, ny, nx
        zz = z + sign * k
        there = pos_of(xx, yy, zz, c)

        def body():
            if act == "start" and (f or s or k):
                copy(there, half, 4, partner).wait_recv()

            def go(kind, target):
                cp = copy(there, half, kind, target)
                if act == "start":
                    cp.start()
                else:
                    cp.wait_send()

            if f == 0 and s == 0:
                if k == 0 or (sign < 0 and k < nz - 1):
                    pl.when(z + 1 < nz)(lambda: go(0, up))
                if k == 0 or (sign > 0 and k < nz - 1):
                    pl.when(z > 0)(lambda: go(1, down))
            if s == 0 and f < nf - 1:
                go(2, first)
            if s < ns - 1:
                go(3, second)
            go(4, partner)

        if k == 0:
            body()
        elif sign < 0:
            pl.when(z >= k)(body)
        else:
            pl.when(z + k < nz)(body)

    def column_stats(rx, ry):
        xx, yy = lax.rem(x - rx + nx, nx), lax.rem(y - ry + ny, ny)
        for zz in range(nz):
            for half in range(2):
                copy(pos_of(xx, yy, zz, 1 - c), half, 4, partner).wait_recv()
        q = xx * ny + yy
        token_rows = pl.ds(pl.multiple_of(q * lanes, lanes), lanes)
        extra = width - depth
        pick = (lax.broadcasted_iota(jnp.int32, (16, extra), 0)
                == lax.broadcasted_iota(jnp.int32, (16, extra), 1))
        digit = lax.dot_general(
            pick.astype(jnp.float32).astype(jnp.bfloat16), g[token_rows, depth:width],
            (((1,), (1,)), ((), ())), preferred_element_type=jnp.float32)
        target = digit[0:1, :] + digit[1:2, :] * 256.0 + digit[2:3, :] * 65536.0
        target = target - (me * vocab).astype(jnp.float32)

        def tile(v, carry):
            peak, mass, hit = carry
            logits = lax.dot_general(
                hbuf[pl.ds(pl.multiple_of(v * vt, vt), vt), :], g[token_rows, 0:depth],
                (((1,), (1,)), ((), ())), preferred_element_type=jnp.float32)
            ids = lax.broadcasted_iota(jnp.int32, (vt, lanes), 0) + v * vt
            top = jnp.maximum(peak, jnp.max(logits, axis=0, keepdims=True))
            mass = mass * jnp.exp(peak - top) + jnp.sum(jnp.exp(logits - top), axis=0, keepdims=True)
            hit = hit + jnp.sum(
                jnp.where(ids.astype(jnp.float32) == target, logits, 0.0), axis=0, keepdims=True)
            return top, mass, hit

        zero = jnp.zeros((1, lanes), jnp.float32)
        peak, mass, hit = lax.fori_loop(
            0, vocab // vt, tile, (jnp.full((1, lanes), -3e38, jnp.float32), zero, zero))
        stat[me, pl.ds(q, 1), :] = peak + jnp.log(mass)
        stat[me, pl.ds(columns + q, 1), :] = hit

    def events():
        found = []
        for k in range(nz):
            for f in range(max(nx, ny)):
                for s in range(max(nx, ny)):
                    found.append((k + f + s, f + s, k, f, s))
        return sorted(found)

    def legal(half, f, s):
        nf, ns = (nx, ny) if half == 0 else (ny, nx)
        return f < nf and s < ns

    def all_events(act, level=None):
        for order, _, k, f, s in events():
            if level is not None and order != level:
                continue
            for half in range(2):
                if legal(half, f, s):
                    for sign in ((-1, 1) if k else (1,)):
                        arrive(half, f, s, k, sign, act)

    last = nz - 1 + nx - 1 + ny - 1
    for level in range(last + 1):
        all_events("start", level)
        if level == nz - 1:
            head_copy.wait()
        if level >= nz - 1:
            for rx in range(nx):
                for ry in range(ny):
                    if rx + ry == level - (nz - 1):
                        column_stats(rx, ry)

    def stat_copy(source, other):
        return pltpu.make_async_remote_copy(
            src_ref=stat.at[source],
            dst_ref=stat.at[source],
            send_sem=stat_send.at[other],
            recv_sem=stat_recv.at[source],
            device_id=(other // npp, lax.rem(other, npp)),
            device_id_type=MESH,
        )

    def send_stat(d, carry):
        stat_copy(me, lax.rem(me + d, devices)).start()
        return carry

    def take_stat(d, carry):
        other = lax.rem(me + d, devices)
        stat_copy(other, other).wait_recv()
        return carry

    def sent_stat(d, carry):
        stat_copy(me, lax.rem(me + d, devices)).wait_send()
        return carry

    lax.fori_loop(1, devices, send_stat, 0)
    all_events("finish")
    lax.fori_loop(1, devices, take_stat, 0)

    every = stat[...]
    top = jnp.max(every[:, 0:columns, :], axis=0)
    mass = jnp.sum(jnp.exp(every[:, 0:columns, :] - top[None]), axis=0)
    loss = top + jnp.log(mass) - jnp.sum(every[:, columns:, :], axis=0)
    loss_ref[...] = loss
    row = jnp.broadcast_to(loss_ref[pl.ds(x * ny + y, 1), :], (8, lanes))
    shift = (z * CORES + c) * rows
    moved = pltpu.roll(row, lax.rem(lanes - shift, lanes), axis=1)
    out_lane = lax.broadcasted_iota(jnp.int32, (8, lanes), 1)
    pipes = jnp.zeros((8, lanes), jnp.float32)
    for p in range(ndp):
        total = jnp.sum(jnp.where(rmap[...] == p, loss, 0.0), keepdims=True)
        pipes = jnp.where(out_lane == p, total / (rows * devices // ndp), pipes)
    out_row = lax.broadcasted_iota(jnp.int32, (8, lanes), 0)
    out[...] = jnp.where(out_row == 0, moved, pipes)
    lax.fori_loop(1, devices, sent_stat, 0)


def shards(geom, hidden, norm_gain, head, targets, route):
    nx, ny, nz, ndp, npp = geom
    devices = ndp * npp
    rows, depth = hidden.shape
    lanes = nz * CORES * rows
    columns = nx * ny
    vmem = pl.BlockSpec(memory_space=pltpu.VMEM)
    out = pl.pallas_call(
        functools.partial(kernel, geom),
        out_shape=jax.ShapeDtypeStruct((8, lanes), jnp.float32),
        in_specs=[vmem, vmem, vmem, pl.BlockSpec(memory_space=pltpu.SMEM),
                  pl.BlockSpec(memory_space=pl.ANY)],
        out_specs=vmem,
        scratch_shapes=[
            pltpu.VMEM((rows * devices, depth + 128), jnp.bfloat16),
            pltpu.VMEM(head.shape, jnp.bfloat16),
            pltpu.VMEM((devices, 2 * columns, lanes), jnp.float32),
            pltpu.VMEM((columns, lanes), jnp.float32),
            pltpu.VMEM((columns, lanes), jnp.int32),
            pltpu.SemaphoreType.DMA((2, devices)),
            pltpu.SemaphoreType.DMA((5, 2, devices // CORES)),
            pltpu.SemaphoreType.DMA((devices,)),
            pltpu.SemaphoreType.DMA((devices,)),
            pltpu.SemaphoreType.DMA,
        ],
        compiler_params=pltpu.CompilerParams(collective_id=0, has_side_effects=True),
    )(hidden, norm_gain.reshape(1, depth), targets.reshape(1, rows), route, head)
    return out[0, :rows], out[1, :ndp]


def solution(mesh):
    ndp, npp = mesh.shape["dp"], mesh.shape["pp"]
    nx = ndp // CORES
    ny = math.gcd(nx, npp)
    geom = (nx, ny, npp // ny, ndp, npp)
    placed = (P(("dp", "pp"), None), P(), P(("dp", "pp"), None), P(("dp", "pp")), P())
    return jax.shard_map(
        functools.partial(shards, geom), mesh=mesh, in_specs=placed,
        out_specs=(P(("dp", "pp")), P()), check_vma=False
    )
```

time: 166 us -> 51 us (0.31)
  blocking collectives: 80.3 us -> 0 us
  Pallas kernels: 0 us -> 47.8 us
  waiting for transfers between devices: 44.3 us -> 0 us
  between operations: 14.1 us -> 0.64 us
  starting transfers between devices: 8.47 us -> 0 us
  matrix products: 7.43 us -> 0 us
  other arithmetic: 6.91 us -> 0 us
    pallas_call x0 -> x1, Pallas kernels: none -> 47.8 us  [shards(): pl.pallas_call(functools.partial(kernel, geom), out_shape=jax.ShapeDtypeS...]
    unnamed x1 -> x0, blocking collectives: 42 us -> none
    psum x1 -> x0, blocking collectives: 38.2 us -> none  [shards(): summed = lax.psum(credit, ('dp', 'pp'))]
    all_gather x1 -> x0, waiting for transfers between devices: 24.9 us -> none  [shards(): lax.all_gather(hidden, ('dp', 'pp'), axis=0, tiled=True)]
    all_to_all x3 -> x0, waiting for transfers between devices: 18.7 us -> none  [the longest x1 7.12 us: shards(): lax.all_to_all(hit.reshape(devices, rows), ('dp', 'pp'), split_axis=0, co...]
    all_to_all x3 -> x0, starting transfers between devices: 8.44 us -> none  [the longest x1 3.39 us: shards(): lax.all_to_all(peak.reshape(devices, rows), ('dp', 'pp'), split_axis=0, c...]
    dot_general x1 -> x0, matrix products: 7.43 us -> none  [one_block(): lax.dot_general(rows, head, (((1,), (1,)), ((), ())), preferred_element_t...]
    reduce_sum x5 -> x0, other arithmetic: 5.05 us -> none  [the longest x1 3.23 us: rms_normal(): factor = lax.rsqrt(jnp.mean(wide * wide, axis=1, keepdims=True) + 1e-05)]
  transfers between devices with their start and end apart: 4 -> 0, of which waited for: 4 -> 0; matrix products, arithmetic and copies ran while one was open for 1% -> 0% of each run, Pallas kernels for 0% -> 0%
where the time goes in v1:
time: 51 us; the launch traced here: 50.8 us
  Pallas kernels  47.8 us (94%)
  local copies, waits for them, and re-layouts  2.39 us (5%)
  between operations  0.64 us (1%)
    pallas_call x1, Pallas kernels, shards(): pl.pallas_call(functools.partial(kernel, geom), out_shape=jax.ShapeDtypeS...  47.8 us
    squeeze x2, local copies, waits for them, and re-layouts, shards(): return (out[0, :rows], out[1, :ndp])  2.39 us

profile of v1, /device:TPU:0, one launch (start us, length us, event | category | flops | bytes accessed | tf_op | source)
XLA Modules:
  0.0 50.8 jit_solution(4088704415956528248)
XLA Ops:
  0.6 47.8 %shard_map.68 = f32[8,128]{1,0:T(8,128)} custom-call(bf16[16,4096]{1,0:T(8,128)(2,1)} %hid.1, f32[1,4096]{1,0:T(1,128)} %bitcast.6, s32[1,16]{1,0:T(1,128)} %bitcast.7, s32[32]{0:T(128)} %route.1, bf16[1024,4096]{1,0:T(8,128)(2,1)} %head.1), custom_call_target="tpu_custom_call" | custom-call | tf_op jit(solution)/shard_map/pallas_call | solution.py:255
  48.4 1.2 %slice_bitcast_fusion = f32[4]{0:T(128)} fusion(f32[8,128]{1,0:T(8,128)} %shard_map.68), kind=kLoop, calls=%fused_computation | loop fusion | bytes 32 | tf_op jit(solution)/shard_map/squeeze | solution.py:275
  49.6 1.2 %slice_bitcast_fusion.1 = f32[16]{0:T(128)} fusion(f32[8,128]{1,0:T(8,128)} %shard_map.68), kind=kLoop, calls=%fused_computation.1 | loop fusion | bytes 128 | tf_op jit(solution)/shard_map/squeeze | solution.py:275
